TPU v7x, 32 devices: a whole 2x2x4 slice. The times are simulated.
32 devices in a mesh: tm: 8 (over z, core), state: 4 (over y, x).
Axes of the slice: x: 2, y: 2, z: 4, core: 2. Of those that a mesh axis runs over, the one named last changes fastest.
Arguments:
- increments: bfloat16 [8, 2048, 128], P('tm', 'state'), may hold values from -4 to 4
- propagators: bfloat16 [8, 2048, 2048], P('tm', 'state'), may hold values from -1.1 to 1.1
- inv_var: float32 [8, 2048], P('tm', 'state'), may hold values from 0.25 to 2
Outputs:
- forward_state: bfloat16 [8, 2048, 128], P('tm', 'state')
- adjoint: bfloat16 [8, 2048, 128], P('tm', 'state')
All inputs are finite; a program needn't handle non-finite values.
Results may differ from a plain program's by a relative error of at most 0.03.
Values may be sent and summed in bfloat16 or wider, within the bound.
A program may use at most 64 MiB of HBM per device.

v0:
```python
import jax
import jax.numpy as jnp
from jax import lax
from jax.sharding import PartitionSpec as P


def passed_along(block, axis, distance):
    devices = range(lax.axis_size(axis))
    route = [(i - distance, i) for i in devices if i - distance in devices]
    return lax.ppermute(block, axis, route)


def per_device(increments, propagators, inv_var):
    matrix = propagators[0]
    driving = increments[0]
    weight = inv_var[0]
    rounds = lax.axis_size("tm") - 1
    driving_wide = driving.astype(jnp.float32)

    def absorb(piece):
        return jnp.dot(matrix, piece, preferred_element_type=jnp.float32)

    def forward_round(step, current):
        arrived = passed_along(current, "tm", 1)
        total = absorb(lax.all_gather(arrived, "state", axis=0, tiled=True))
        return (total + driving_wide).astype(jnp.bfloat16)

    forward_state = lax.fori_loop(0, rounds, forward_round, driving)
    weighted = weight[:, None] * forward_state.astype(jnp.float32)
    columns = lax.all_to_all(matrix, "state", split_axis=1, concat_axis=0, tiled=True)

    def column_absorb(piece):
        return lax.dot_general(
            columns, piece, (((0,), (0,)), ((), ())), preferred_element_type=jnp.float32
        )

    def carry_term(current):
        return column_absorb(lax.all_gather(current, "state", axis=0, tiled=True))

    def backward_round(step, current):
        produced = carry_term(current)
        arrived = passed_along(produced.astype(jnp.bfloat16), "tm", -1).astype(produced.dtype)
        return (weighted + arrived).astype(jnp.bfloat16)

    adjoint = lax.fori_loop(0, rounds, backward_round, weighted.astype(jnp.bfloat16))
    return (forward_state[None], adjoint[None])


def solution(mesh):
    in_specs = (P("tm", "state", None), P("tm", "state", None), P("tm", "state"))
    out_specs = (P("tm", "state", None), P("tm", "state", None))
    return jax.shard_map(
        per_device, mesh=mesh, in_specs=in_specs, out_specs=out_specs, check_vma=False
    )
```

profile of v0, /device:TPU:0, one launch (start us, length us, event | category | flops | bytes accessed | tf_op | source)
XLA Modules:
  0.0 267.9 jit_solution(13853692734291868229)
XLA Ops:
  1.5 3.3 %all_to_all.14 = bf16[512,4,512]{2,1,0:T(4,128)(2,1)S(1)} reshape(bf16[1,512,2048]{2,1,0:T(8,128)(2,1)} %param.8) | data formatting | bytes 4194304 | tf_op jit(solution)/shard_map/all_to_all | solution.py:30
  4.9 1.7 copy.5
  6.6 5.3 %all-to-all-start = ((bf16[512,4,512]{2,0,1:T(8,128)(2,1)}), bf16[512,4,512]{2,0,1:T(8,128)(2,1)}, u32[]{:S(2)}, u32[]{:S(2)}) async-start(bf16[512,4,512]{2,0,1:T(8,128)(2,1)} %copy.5), calls=%async_computation | async-start | bytes 4194304 | tf_op jit(solution)/shard_map/all_to_all | solution.py:30
  12.0 128.3 %while.20 = (s32[]{:T(128)}, bf16[512,128]{1,0:T(8,128)(2,1)S(1)}, bf16[512,2048]{1,0:T(8,128)(2,1)S(1)}, f32[512,128]{1,0:T(8,128)S(1)}, s32[]{:T(128)}) while((s32[]{:T(128)}, bf16[512,128]{1,0:T(8,128)(2,1)S(1)}, bf16[512,2048]{1,0:T(8,128)(2,1)S(1)}, f32[512,128]{1,0:T(8,128)S(1)}, s32[]{:T(128)}) %tuple.43), condition=%wide.region_1.0_spmd, body=%wide.region_0.0_spmd.sunk | while | flops 268566528 | bytes 4194405 | solution.py:28
  12.0 1.7 collective-permute-start
  14.6 28.9 %all_gather.8 = bf16[2048,128]{1,0:T(8,128)(2,1)S(1)} all-gather(bf16[512,128]{1,0:T(8,128)(2,1)S(1)} %collective-permute-done), channel_id=1, replica_groups=mesh['tm'=8,'state'=4] {'state'}, dimensions={0}, use_global_device_ids=true | all-gather | bytes 655360 | tf_op jit(solution)/shard_map/while/body/eval_jaxpr/all_gather | solution.py:25
  44.2 1.3 collective-permute-start
  45.5 1.0 collective-permute-done
  46.5 9.6 %all_gather.8 = bf16[2048,128]{1,0:T(8,128)(2,1)S(1)} all-gather(bf16[512,128]{1,0:T(8,128)(2,1)S(1)} %collective-permute-done), channel_id=1, replica_groups=mesh['tm'=8,'state'=4] {'state'}, dimensions={0}, use_global_device_ids=true | all-gather | bytes 655360 | tf_op jit(solution)/shard_map/while/body/eval_jaxpr/all_gather | solution.py:25
  56.7 3.0 %collective-permute-start = (bf16[512,128]{1,0:T(8,128)(2,1)S(1)}, bf16[512,128]{1,0:T(8,128)(2,1)S(1)}, u32[]{:S(2)}, u32[]{:S(2)}) collective-permute-start(bf16[512,128]{1,0:T(8,128)(2,1)S(1)} %get-tuple-element.122), channel_id=1, source_target_pairs={{0,4},{4,8},{8,12},{12,16},{16,20},{20,24},{24,28},{1,5},{5,9},{9,... | collective-permute-start | bytes 393224 | tf_op jit(solution)/shard_map/while/body/eval_jaxpr/ppermute | solution.py:10
  60.7 11.1 %all_gather.8 = bf16[2048,128]{1,0:T(8,128)(2,1)S(1)} all-gather(bf16[512,128]{1,0:T(8,128)(2,1)S(1)} %collective-permute-done), channel_id=1, replica_groups=mesh['tm'=8,'state'=4] {'state'}, dimensions={0}, use_global_device_ids=true | all-gather | bytes 655360 | tf_op jit(solution)/shard_map/while/body/eval_jaxpr/all_gather | solution.py:25
  72.5 4.5 %collective-permute-start = (bf16[512,128]{1,0:T(8,128)(2,1)S(1)}, bf16[512,128]{1,0:T(8,128)(2,1)S(1)}, u32[]{:S(2)}, u32[]{:S(2)}) collective-permute-start(bf16[512,128]{1,0:T(8,128)(2,1)S(1)} %get-tuple-element.122), channel_id=1, source_target_pairs={{0,4},{4,8},{8,12},{12,16},{16,20},{20,24},{24,28},{1,5},{5,9},{9,... | collective-permute-start | bytes 393224 | tf_op jit(solution)/shard_map/while/body/eval_jaxpr/ppermute | solution.py:10
  78.0 9.8 %all_gather.8 = bf16[2048,128]{1,0:T(8,128)(2,1)S(1)} all-gather(bf16[512,128]{1,0:T(8,128)(2,1)S(1)} %collective-permute-done), channel_id=1, replica_groups=mesh['tm'=8,'state'=4] {'state'}, dimensions={0}, use_global_device_ids=true | all-gather | bytes 655360 | tf_op jit(solution)/shard_map/while/body/eval_jaxpr/all_gather | solution.py:25
  88.5 5.3 %collective-permute-start = (bf16[512,128]{1,0:T(8,128)(2,1)S(1)}, bf16[512,128]{1,0:T(8,128)(2,1)S(1)}, u32[]{:S(2)}, u32[]{:S(2)}) collective-permute-start(bf16[512,128]{1,0:T(8,128)(2,1)S(1)} %get-tuple-element.122), channel_id=1, source_target_pairs={{0,4},{4,8},{8,12},{12,16},{16,20},{20,24},{24,28},{1,5},{5,9},{9,... | collective-permute-start | bytes 393224 | tf_op jit(solution)/shard_map/while/body/eval_jaxpr/ppermute | solution.py:10
  94.8 10.3 %all_gather.8 = bf16[2048,128]{1,0:T(8,128)(2,1)S(1)} all-gather(bf16[512,128]{1,0:T(8,128)(2,1)S(1)} %collective-permute-done), channel_id=1, replica_groups=mesh['tm'=8,'state'=4] {'state'}, dimensions={0}, use_global_device_ids=true | all-gather | bytes 655360 | tf_op jit(solution)/shard_map/while/body/eval_jaxpr/all_gather | solution.py:25
  105.8 5.8 %collective-permute-start = (bf16[512,128]{1,0:T(8,128)(2,1)S(1)}, bf16[512,128]{1,0:T(8,128)(2,1)S(1)}, u32[]{:S(2)}, u32[]{:S(2)}) collective-permute-start(bf16[512,128]{1,0:T(8,128)(2,1)S(1)} %get-tuple-element.122), channel_id=1, source_target_pairs={{0,4},{4,8},{8,12},{12,16},{16,20},{20,24},{24,28},{1,5},{5,9},{9,... | collective-permute-start | bytes 393224 | tf_op jit(solution)/shard_map/while/body/eval_jaxpr/ppermute | solution.py:10
  112.5 9.0 %all_gather.8 = bf16[2048,128]{1,0:T(8,128)(2,1)S(1)} all-gather(bf16[512,128]{1,0:T(8,128)(2,1)S(1)} %collective-permute-done), channel_id=1, replica_groups=mesh['tm'=8,'state'=4] {'state'}, dimensions={0}, use_global_device_ids=true | all-gather | bytes 655360 | tf_op jit(solution)/shard_map/while/body/eval_jaxpr/all_gather | solution.py:25
  122.3 6.0 %collective-permute-start = (bf16[512,128]{1,0:T(8,128)(2,1)S(1)}, bf16[512,128]{1,0:T(8,128)(2,1)S(1)}, u32[]{:S(2)}, u32[]{:S(2)}) collective-permute-start(bf16[512,128]{1,0:T(8,128)(2,1)S(1)} %get-tuple-element.122), channel_id=1, source_target_pairs={{0,4},{4,8},{8,12},{12,16},{16,20},{20,24},{24,28},{1,5},{5,9},{9,... | collective-permute-start | bytes 393224 | tf_op jit(solution)/shard_map/while/body/eval_jaxpr/ppermute | solution.py:10
  129.3 10.3 %all_gather.8 = bf16[2048,128]{1,0:T(8,128)(2,1)S(1)} all-gather(bf16[512,128]{1,0:T(8,128)(2,1)S(1)} %collective-permute-done), channel_id=1, replica_groups=mesh['tm'=8,'state'=4] {'state'}, dimensions={0}, use_global_device_ids=true | all-gather | bytes 655360 | tf_op jit(solution)/shard_map/while/body/eval_jaxpr/all_gather | solution.py:25
  140.9 126.3 %while.21 = (s32[]{:T(128)}, bf16[512,128]{1,0:T(8,128)(2,1)S(1)}, bf16[2048,512]{1,0:T(8,128)(2,1)}, f32[512,128]{1,0:T(8,128)S(1)}, s32[]{:T(128)}) while((s32[]{:T(128)}, bf16[512,128]{1,0:T(8,128)(2,1)S(1)}, bf16[2048,512]{1,0:T(8,128)(2,1)}, f32[512,128]{1,0:T(8,128)S(1)}, s32[]{:T(128)}) %tuple.39), condition=%wide.region_3.0_spmd, body=%wide.region_2.0_spmd.sunk | while | flops 268697600 | bytes 4456549 | solution.py:45
  140.9 9.5 %all_gather.9 = bf16[2048,128]{1,0:T(8,128)(2,1)S(1)} all-gather(bf16[512,128]{1,0:T(8,128)(2,1)S(1)} %get-tuple-element.137), channel_id=1, replica_groups=mesh['tm'=8,'state'=4] {'state'}, dimensions={0}, use_global_device_ids=true | all-gather | bytes 655360 | tf_op jit(solution)/shard_map/while/body/eval_jaxpr/all_gather | solution.py:38
  150.4 2.3 convolution_convert_fusion.2
  152.8 1.3 collective-permute-start.1
  154.1 3.2 %collective-permute-done.1 = bf16[512,128]{1,0:T(8,128)(2,1)S(1)} collective-permute-done((bf16[512,128]{1,0:T(8,128)(2,1)S(1)}, bf16[512,128]{1,0:T(8,128)(2,1)S(1)}, u32[]{:S(2)}, u32[]{:S(2)}) %collective-permute-start.1) | collective-permute-done | bytes 131104 | tf_op jit(solution)/shard_map/while/body/eval_jaxpr/ppermute | solution.py:10
  157.3 10.7 %all_gather.9 = bf16[2048,128]{1,0:T(8,128)(2,1)S(1)} all-gather(bf16[512,128]{1,0:T(8,128)(2,1)S(1)} %get-tuple-element.137), channel_id=1, replica_groups=mesh['tm'=8,'state'=4] {'state'}, dimensions={0}, use_global_device_ids=true | all-gather | bytes 655360 | tf_op jit(solution)/shard_map/while/body/eval_jaxpr/all_gather | solution.py:38
  168.0 2.3 convolution_convert_fusion.2
  170.3 1.3 collective-permute-start.1
  171.6 7.7 %collective-permute-done.1 = bf16[512,128]{1,0:T(8,128)(2,1)S(1)} collective-permute-done((bf16[512,128]{1,0:T(8,128)(2,1)S(1)}, bf16[512,128]{1,0:T(8,128)(2,1)S(1)}, u32[]{:S(2)}, u32[]{:S(2)}) %collective-permute-start.1) | collective-permute-done | bytes 131104 | tf_op jit(solution)/shard_map/while/body/eval_jaxpr/ppermute | solution.py:10
  179.4 9.5 %all_gather.9 = bf16[2048,128]{1,0:T(8,128)(2,1)S(1)} all-gather(bf16[512,128]{1,0:T(8,128)(2,1)S(1)} %get-tuple-element.137), channel_id=1, replica_groups=mesh['tm'=8,'state'=4] {'state'}, dimensions={0}, use_global_device_ids=true | all-gather | bytes 655360 | tf_op jit(solution)/shard_map/while/body/eval_jaxpr/all_gather | solution.py:38
  188.9 2.3 convolution_convert_fusion.2
  191.3 1.3 collective-permute-start.1
  192.6 3.7 %collective-permute-done.1 = bf16[512,128]{1,0:T(8,128)(2,1)S(1)} collective-permute-done((bf16[512,128]{1,0:T(8,128)(2,1)S(1)}, bf16[512,128]{1,0:T(8,128)(2,1)S(1)}, u32[]{:S(2)}, u32[]{:S(2)}) %collective-permute-start.1) | collective-permute-done | bytes 131104 | tf_op jit(solution)/shard_map/while/body/eval_jaxpr/ppermute | solution.py:10
  196.3 10.4 %all_gather.9 = bf16[2048,128]{1,0:T(8,128)(2,1)S(1)} all-gather(bf16[512,128]{1,0:T(8,128)(2,1)S(1)} %get-tuple-element.137), channel_id=1, replica_groups=mesh['tm'=8,'state'=4] {'state'}, dimensions={0}, use_global_device_ids=true | all-gather | bytes 655360 | tf_op jit(solution)/shard_map/while/body/eval_jaxpr/all_gather | solution.py:38
  206.8 2.3 convolution_convert_fusion.2
  209.1 1.3 collective-permute-start.1
  210.4 3.6 %collective-permute-done.1 = bf16[512,128]{1,0:T(8,128)(2,1)S(1)} collective-permute-done((bf16[512,128]{1,0:T(8,128)(2,1)S(1)}, bf16[512,128]{1,0:T(8,128)(2,1)S(1)}, u32[]{:S(2)}, u32[]{:S(2)}) %collective-permute-start.1) | collective-permute-done | bytes 131104 | tf_op jit(solution)/shard_map/while/body/eval_jaxpr/ppermute | solution.py:10
  214.1 10.1 %all_gather.9 = bf16[2048,128]{1,0:T(8,128)(2,1)S(1)} all-gather(bf16[512,128]{1,0:T(8,128)(2,1)S(1)} %get-tuple-element.137), channel_id=1, replica_groups=mesh['tm'=8,'state'=4] {'state'}, dimensions={0}, use_global_device_ids=true | all-gather | bytes 655360 | tf_op jit(solution)/shard_map/while/body/eval_jaxpr/all_gather | solution.py:38
  224.2 2.3 convolution_convert_fusion.2
  226.5 1.3 collective-permute-start.1
  227.8 4.2 %collective-permute-done.1 = bf16[512,128]{1,0:T(8,128)(2,1)S(1)} collective-permute-done((bf16[512,128]{1,0:T(8,128)(2,1)S(1)}, bf16[512,128]{1,0:T(8,128)(2,1)S(1)}, u32[]{:S(2)}, u32[]{:S(2)}) %collective-permute-start.1) | collective-permute-done | bytes 131104 | tf_op jit(solution)/shard_map/while/body/eval_jaxpr/ppermute | solution.py:10
  232.0 9.6 %all_gather.9 = bf16[2048,128]{1,0:T(8,128)(2,1)S(1)} all-gather(bf16[512,128]{1,0:T(8,128)(2,1)S(1)} %get-tuple-element.137), channel_id=1, replica_groups=mesh['tm'=8,'state'=4] {'state'}, dimensions={0}, use_global_device_ids=true | all-gather | bytes 655360 | tf_op jit(solution)/shard_map/while/body/eval_jaxpr/all_gather | solution.py:38
  241.6 2.4 convolution_convert_fusion.2
  244.0 1.3 collective-permute-start.1
  245.3 3.6 %collective-permute-done.1 = bf16[512,128]{1,0:T(8,128)(2,1)S(1)} collective-permute-done((bf16[512,128]{1,0:T(8,128)(2,1)S(1)}, bf16[512,128]{1,0:T(8,128)(2,1)S(1)}, u32[]{:S(2)}, u32[]{:S(2)}) %collective-permute-start.1) | collective-permute-done | bytes 131104 | tf_op jit(solution)/shard_map/while/body/eval_jaxpr/ppermute | solution.py:10
  248.9 10.5 %all_gather.9 = bf16[2048,128]{1,0:T(8,128)(2,1)S(1)} all-gather(bf16[512,128]{1,0:T(8,128)(2,1)S(1)} %get-tuple-element.137), channel_id=1, replica_groups=mesh['tm'=8,'state'=4] {'state'}, dimensions={0}, use_global_device_ids=true | all-gather | bytes 655360 | tf_op jit(solution)/shard_map/while/body/eval_jaxpr/all_gather | solution.py:38
  259.4 2.3 convolution_convert_fusion.2
  261.7 1.3 collective-permute-start.1
  263.0 4.2 %collective-permute-done.1 = bf16[512,128]{1,0:T(8,128)(2,1)S(1)} collective-permute-done((bf16[512,128]{1,0:T(8,128)(2,1)S(1)}, bf16[512,128]{1,0:T(8,128)(2,1)S(1)}, u32[]{:S(2)}, u32[]{:S(2)}) %collective-permute-start.1) | collective-permute-done | bytes 131104 | tf_op jit(solution)/shard_map/while/body/eval_jaxpr/ppermute | solution.py:10
  (32 shorter events, 13.2 us)
Async XLA Ops:
  6.6 5.3 %copy-start = (bf16[1,512,2048]{2,1,0:T(8,128)(2,1)S(1)}, bf16[1,512,2048]{2,1,0:T(8,128)(2,1)}, u32[]{:S(2)}) copy-start(bf16[1,512,2048]{2,1,0:T(8,128)(2,1)} %param.8) | copy-start | bytes 6291460
  6.6 133.8 %all-to-all-start = ((bf16[512,4,512]{2,0,1:T(8,128)(2,1)}), bf16[512,4,512]{2,0,1:T(8,128)(2,1)}, u32[]{:S(2)}, u32[]{:S(2)}) async-start(bf16[512,4,512]{2,0,1:T(8,128)(2,1)} %copy.5), calls=%async_computation | async-start | bytes 4194304 | tf_op jit(solution)/shard_map/all_to_all | solution.py:30
  11.9 128.3 %copy-start.3 = (f32[1,512]{1,0:T(1,128)S(1)}, f32[1,512]{1,0:T(1,128)}, u32[]{:S(2)}) copy-start(f32[1,512]{1,0:T(1,128)} %param.9) | copy-start | bytes 6148
  12.0 2.6 collective-permute-start
  44.2 2.3 collective-permute-start
  56.7 3.9 %collective-permute-start = (bf16[512,128]{1,0:T(8,128)(2,1)S(1)}, bf16[512,128]{1,0:T(8,128)(2,1)S(1)}, u32[]{:S(2)}, u32[]{:S(2)}) collective-permute-start(bf16[512,128]{1,0:T(8,128)(2,1)S(1)} %get-tuple-element.122), channel_id=1, source_target_pairs={{0,4},{4,8},{8,12},{12,16},{16,20},{20,24},{24,28},{1,5},{5,9},{9,... | collective-permute-start | bytes 393224 | tf_op jit(solution)/shard_map/while/body/eval_jaxpr/ppermute | solution.py:10
  72.5 5.5 %collective-permute-start = (bf16[512,128]{1,0:T(8,128)(2,1)S(1)}, bf16[512,128]{1,0:T(8,128)(2,1)S(1)}, u32[]{:S(2)}, u32[]{:S(2)}) collective-permute-start(bf16[512,128]{1,0:T(8,128)(2,1)S(1)} %get-tuple-element.122), channel_id=1, source_target_pairs={{0,4},{4,8},{8,12},{12,16},{16,20},{20,24},{24,28},{1,5},{5,9},{9,... | collective-permute-start | bytes 393224 | tf_op jit(solution)/shard_map/while/body/eval_jaxpr/ppermute | solution.py:10
  88.5 6.2 %collective-permute-start = (bf16[512,128]{1,0:T(8,128)(2,1)S(1)}, bf16[512,128]{1,0:T(8,128)(2,1)S(1)}, u32[]{:S(2)}, u32[]{:S(2)}) collective-permute-start(bf16[512,128]{1,0:T(8,128)(2,1)S(1)} %get-tuple-element.122), channel_id=1, source_target_pairs={{0,4},{4,8},{8,12},{12,16},{16,20},{20,24},{24,28},{1,5},{5,9},{9,... | collective-permute-start | bytes 393224 | tf_op jit(solution)/shard_map/while/body/eval_jaxpr/ppermute | solution.py:10
  105.8 6.8 %collective-permute-start = (bf16[512,128]{1,0:T(8,128)(2,1)S(1)}, bf16[512,128]{1,0:T(8,128)(2,1)S(1)}, u32[]{:S(2)}, u32[]{:S(2)}) collective-permute-start(bf16[512,128]{1,0:T(8,128)(2,1)S(1)} %get-tuple-element.122), channel_id=1, source_target_pairs={{0,4},{4,8},{8,12},{12,16},{16,20},{20,24},{24,28},{1,5},{5,9},{9,... | collective-permute-start | bytes 393224 | tf_op jit(solution)/shard_map/while/body/eval_jaxpr/ppermute | solution.py:10
  122.3 7.0 %collective-permute-start = (bf16[512,128]{1,0:T(8,128)(2,1)S(1)}, bf16[512,128]{1,0:T(8,128)(2,1)S(1)}, u32[]{:S(2)}, u32[]{:S(2)}) collective-permute-start(bf16[512,128]{1,0:T(8,128)(2,1)S(1)} %get-tuple-element.122), channel_id=1, source_target_pairs={{0,4},{4,8},{8,12},{12,16},{16,20},{20,24},{24,28},{1,5},{5,9},{9,... | collective-permute-start | bytes 393224 | tf_op jit(solution)/shard_map/while/body/eval_jaxpr/ppermute | solution.py:10
  140.2 0.7 copy-start.2
  152.8 4.5 %collective-permute-start.1 = (bf16[512,128]{1,0:T(8,128)(2,1)S(1)}, bf16[512,128]{1,0:T(8,128)(2,1)S(1)}, u32[]{:S(2)}, u32[]{:S(2)}) collective-permute-start(bf16[512,128]{1,0:T(8,128)(2,1)S(1)} %convolution_convert_fusion.2), channel_id=1, source_target_pairs={{4,0},{8,4},{12,8},{16,12},{20,16},{24,20},{28,24},{5,1},{9,5},{13... | collective-permute-start | bytes 393224 | tf_op jit(solution)/shard_map/while/body/eval_jaxpr/ppermute | solution.py:10
  170.3 9.0 %collective-permute-start.1 = (bf16[512,128]{1,0:T(8,128)(2,1)S(1)}, bf16[512,128]{1,0:T(8,128)(2,1)S(1)}, u32[]{:S(2)}, u32[]{:S(2)}) collective-permute-start(bf16[512,128]{1,0:T(8,128)(2,1)S(1)} %convolution_convert_fusion.2), channel_id=1, source_target_pairs={{4,0},{8,4},{12,8},{16,12},{20,16},{24,20},{28,24},{5,1},{9,5},{13... | collective-permute-start | bytes 393224 | tf_op jit(solution)/shard_map/while/body/eval_jaxpr/ppermute | solution.py:10
  191.3 5.0 %collective-permute-start.1 = (bf16[512,128]{1,0:T(8,128)(2,1)S(1)}, bf16[512,128]{1,0:T(8,128)(2,1)S(1)}, u32[]{:S(2)}, u32[]{:S(2)}) collective-permute-start(bf16[512,128]{1,0:T(8,128)(2,1)S(1)} %convolution_convert_fusion.2), channel_id=1, source_target_pairs={{4,0},{8,4},{12,8},{16,12},{20,16},{24,20},{28,24},{5,1},{9,5},{13... | collective-permute-start | bytes 393224 | tf_op jit(solution)/shard_map/while/body/eval_jaxpr/ppermute | solution.py:10
  209.1 4.9 %collective-permute-start.1 = (bf16[512,128]{1,0:T(8,128)(2,1)S(1)}, bf16[512,128]{1,0:T(8,128)(2,1)S(1)}, u32[]{:S(2)}, u32[]{:S(2)}) collective-permute-start(bf16[512,128]{1,0:T(8,128)(2,1)S(1)} %convolution_convert_fusion.2), channel_id=1, source_target_pairs={{4,0},{8,4},{12,8},{16,12},{20,16},{24,20},{28,24},{5,1},{9,5},{13... | collective-permute-start | bytes 393224 | tf_op jit(solution)/shard_map/while/body/eval_jaxpr/ppermute | solution.py:10
  226.5 5.5 %collective-permute-start.1 = (bf16[512,128]{1,0:T(8,128)(2,1)S(1)}, bf16[512,128]{1,0:T(8,128)(2,1)S(1)}, u32[]{:S(2)}, u32[]{:S(2)}) collective-permute-start(bf16[512,128]{1,0:T(8,128)(2,1)S(1)} %convolution_convert_fusion.2), channel_id=1, source_target_pairs={{4,0},{8,4},{12,8},{16,12},{20,16},{24,20},{28,24},{5,1},{9,5},{13... | collective-permute-start | bytes 393224 | tf_op jit(solution)/shard_map/while/body/eval_jaxpr/ppermute | solution.py:10
  244.0 4.9 %collective-permute-start.1 = (bf16[512,128]{1,0:T(8,128)(2,1)S(1)}, bf16[512,128]{1,0:T(8,128)(2,1)S(1)}, u32[]{:S(2)}, u32[]{:S(2)}) collective-permute-start(bf16[512,128]{1,0:T(8,128)(2,1)S(1)} %convolution_convert_fusion.2), channel_id=1, source_target_pairs={{4,0},{8,4},{12,8},{16,12},{20,16},{24,20},{28,24},{5,1},{9,5},{13... | collective-permute-start | bytes 393224 | tf_op jit(solution)/shard_map/while/body/eval_jaxpr/ppermute | solution.py:10
  261.7 5.5 %collective-permute-start.1 = (bf16[512,128]{1,0:T(8,128)(2,1)S(1)}, bf16[512,128]{1,0:T(8,128)(2,1)S(1)}, u32[]{:S(2)}, u32[]{:S(2)}) collective-permute-start(bf16[512,128]{1,0:T(8,128)(2,1)S(1)} %convolution_convert_fusion.2), channel_id=1, source_target_pairs={{4,0},{8,4},{12,8},{16,12},{20,16},{24,20},{28,24},{5,1},{9,5},{13... | collective-permute-start | bytes 393224 | tf_op jit(solution)/shard_map/while/body/eval_jaxpr/ppermute | solution.py:10
  267.3 0.7 copy-start.1
where the time goes:
time: 273 us; the launch traced here: 268 us
  blocking collectives  159 us (58%)
  starting transfers between devices  41.9 us (15%)
  waiting for transfers between devices  36.9 us (14%)
  matrix products  21.5 us (8%)
  local copies, waits for them, and re-layouts  7.1 us (3%)
    all_gather x7, blocking collectives, forward_round(): total = absorb(lax.all_gather(arrived, 'state', axis=0, tiled=True))  88.8 us
    all_gather x7, blocking collectives, carry_term(): return column_absorb(lax.all_gather(current, 'state', axis=0, tiled=True))  70.2 us
    ppermute x14, waiting for transfers between devices, passed_along(): return lax.ppermute(block, axis, route)  36.9 us
    ppermute x14, starting transfers between devices, passed_along(): return lax.ppermute(block, axis, route)  36.6 us
    dot_general x7, matrix products, column_absorb(): lax.dot_general(columns, piece, (((0,), (0,)), ((), ())), preferred_eleme...  16.4 us
  transfers between devices with their start and end apart: 15, of which 14 were waited for; matrix products, arithmetic and copies ran while one was open for 2% of the time, Pallas kernels for 0%

commit v1 on v0

v1 whole, which is shorter than its diff:
```python
import functools

import jax
import jax.numpy as jnp
from jax import lax
from jax.experimental import pallas as pl
from jax.experimental.pallas import tpu as pltpu
from jax.sharding import PartitionSpec as P

MESH = pl.DeviceIdType.MESH
CHUNK = 32


def partner(s, d, n):
    if n & (n - 1):
        return lax.rem(s + d, n)
    bit, out = 1, s
    while bit < n:
        if d & bit:
            out = out + bit - 2 * bit * lax.rem(s // bit, 2)
        bit *= 2
    return out


def kernel(T, n, C, inc_ref, p_hbm, w_ref, f_ref, a_ref, p, pt, x, r, q, p_sem, fs, fr, bs, br):
    t, s = lax.axis_index("tm"), lax.axis_index("state")
    rows, dim = p.shape
    parts = p_sem.shape[0]
    part = rows // parts

    def load(i):
        cut = pl.ds(i * part, part)
        return pltpu.make_async_copy(p_hbm.at[0, cut, :], p.at[cut, :], p_sem.at[i])

    for i in range(parts):
        load(i).start()

    def neighbours(fn):
        @pl.when(t > 0)
        def _():
            fn(t - 1)

        @pl.when(t < T - 1)
        def _():
            fn(t + 1)

    barrier = pltpu.get_barrier_semaphore()

    def greet(other):
        for j in range(n):
            pl.semaphore_signal(barrier, inc=1, device_id=(other, j), device_id_type=MESH)

    neighbours(greet)
    turned = inc_ref[0].T
    for c in range(C):
        f_ref[c] = turned[c * CHUNK:(c + 1) * CHUNK, :]
    middle = jnp.logical_and(t > 0, t < T - 1)

    @pl.when(middle)
    def _():
        pl.semaphore_wait(barrier, 2 * n)

    @pl.when(jnp.logical_not(middle))
    def _():
        pl.semaphore_wait(barrier, n)

    def forward_copy(c, d, index, to):
        return pltpu.make_async_remote_copy(
            src_ref=f_ref.at[c], dst_ref=x.at[c, index], send_sem=fs.at[c, d],
            recv_sem=fr.at[c, index], device_id=to, device_id_type=MESH)

    def backward_copy(c, d, index, to):
        return pltpu.make_async_remote_copy(
            src_ref=q.at[c, d], dst_ref=r.at[c, index], send_sem=bs.at[c, d],
            recv_sem=br.at[c, index], device_id=to, device_id_type=MESH)

    def forward_send(c):
        @pl.when(t < T - 1)
        def _():
            for d in reversed(range(n)):
                forward_copy(c, d, s, (t + 1, partner(s, d, n))).start()

    def backward(c, last):
        weighted = w_ref[...] * f_ref[c].astype(jnp.float32)
        if not last:
            for d in range(n):
                j = partner(s, d, n)
                backward_copy(c, d, j, (t, s)).wait_recv()
                weighted += r[c, j].astype(jnp.float32)
        current = weighted.astype(jnp.bfloat16)
        a_ref[c] = current

        @pl.when(t > 0)
        def _():
            for d in reversed(range(n)):
                j = partner(s, d, n)
                cut = pl.ds(pl.multiple_of(j * rows, rows), rows)
                term = jnp.dot(current, p[:, cut], preferred_element_type=jnp.float32)
                q[c, d] = term.astype(jnp.bfloat16)
                backward_copy(c, d, s, (t - 1, j)).start()

    @pl.when(t == 0)
    def _():
        @pl.loop(0, C)
        def _(c):
            forward_send(c)

        for i in range(parts):
            load(i).wait()

    @pl.when(t > 0)
    def _():
        for i in range(parts):
            load(i).wait()
        block = 128

        @pl.loop(0, dim // block)
        def _(i):
            cut = pl.ds(pl.multiple_of(i * block, block), block)
            pt[cut, :] = p[:, cut].T

        @pl.loop(0, C)
        def _(c):
            total = f_ref[c].astype(jnp.float32)
            for d in range(n):
                j = partner(s, d, n)
                forward_copy(c, d, j, (t, s)).wait_recv()
                cut = pl.ds(pl.multiple_of(j * rows, rows), rows)
                total += jnp.dot(x[c, j], pt[cut, :], preferred_element_type=jnp.float32)
            f_ref[c] = total.astype(jnp.bfloat16)
            forward_send(c)

            @pl.when(t == T - 1)
            def _():
                backward(c, True)

    @pl.when(t < T - 1)
    def _():
        @pl.loop(0, C)
        def _(c):
            backward(c, False)

    @pl.loop(0, C)
    def _(c):
        for d in range(n):
            @pl.when(t < T - 1)
            def _():
                forward_copy(c, d, s, (t, s)).wait_send()

            @pl.when(t > 0)
            def _():
                backward_copy(c, d, s, (t, s)).wait_send()


def solution(mesh):
    T, n = mesh.shape["tm"], mesh.shape["state"]

    def step(increments, propagators, inv_var):
        _, rows, cols = increments.shape
        dim = propagators.shape[2]
        C = cols // CHUNK
        out = jax.ShapeDtypeStruct((C, CHUNK, rows), jnp.bfloat16)
        vmem = pl.BlockSpec(memory_space=pltpu.VMEM)
        f, a = pl.pallas_call(
            functools.partial(kernel, T, n, C),
            out_shape=(out, out),
            in_specs=[vmem, pl.BlockSpec(memory_space=pl.ANY), vmem],
            out_specs=(vmem, vmem),
            scratch_shapes=[
                pltpu.VMEM((rows, dim), jnp.bfloat16),
                pltpu.VMEM((dim, rows), jnp.bfloat16),
                pltpu.VMEM((C, n, CHUNK, rows), jnp.bfloat16),
                pltpu.VMEM((C, n, CHUNK, rows), jnp.bfloat16),
                pltpu.VMEM((C, n, CHUNK, rows), jnp.bfloat16),
                pltpu.SemaphoreType.DMA((4,)),
                pltpu.SemaphoreType.DMA((C, n)),
                pltpu.SemaphoreType.DMA((C, n)),
                pltpu.SemaphoreType.DMA((C, n)),
                pltpu.SemaphoreType.DMA((C, n)),
            ],
            compiler_params=pltpu.CompilerParams(collective_id=0, has_side_effects=True),
        )(increments, propagators, inv_var)
        return (f.reshape(cols, rows).T[None], a.reshape(cols, rows).T[None])

    return jax.shard_map(
        step, mesh=mesh,
        in_specs=(P("tm", "state", None), P("tm", "state", None), P("tm", "state")),
        out_specs=(P("tm", "state", None), P("tm", "state", None)), check_vma=False)
```

time: 273 us -> 67.9 us (0.25); the launches traced: 268 us -> 67.7 us
  blocking collectives: 159 us -> 0 us
  Pallas kernels: 0 us -> 63.7 us
  starting transfers between devices: 41.9 us -> 0 us
  waiting for transfers between devices: 36.9 us -> 0 us
  matrix products: 21.5 us -> 0 us
  local copies, waits for them, and re-layouts: 7.1 us -> 3.33 us
    all_gather x14 -> x0, blocking collectives: 159 us -> none  [the longest x7 88.8 us: forward_round(): total = absorb(lax.all_gather(arrived, 'state', axis=0, tiled=True))]
    pallas_call x0 -> x1, Pallas kernels: none -> 63.7 us  [step(): pl.pallas_call(functools.partial(kernel, T, n, C), out_shape=(out, out),...]
    ppermute x14 -> x0, waiting for transfers between devices: 36.9 us -> none  [passed_along(): return lax.ppermute(block, axis, route)]
    ppermute x14 -> x0, starting transfers between devices: 36.6 us -> none  [passed_along(): return lax.ppermute(block, axis, route)]
    dot_general x14 -> x0, matrix products: 21.5 us -> none  [the longest x7 16.4 us: column_absorb(): lax.dot_general(columns, piece, (((0,), (0,)), ((), ())), preferred_eleme...]
    all_to_all x1 -> x0, starting transfers between devices: 5.32 us -> none  [per_device(): lax.all_to_all(matrix, 'state', split_axis=1, concat_axis=0, tiled=True)]
    all_to_all x2 -> x0, local copies, waits for them, and re-layouts: 5.04 us -> none  [per_device(): lax.all_to_all(matrix, 'state', split_axis=1, concat_axis=0, tiled=True)]
    reshape x0 -> x2, local copies, waits for them, and re-layouts: none -> 3.33 us  [step(): return (f.reshape(cols, rows).T[None], a.reshape(cols, rows).T[None])]
  transfers between devices with their start and end apart: 15 -> 0, of which waited for: 14 -> 0; matrix products, arithmetic and copies ran while one was open for 2% -> 0% of each run, Pallas kernels for 0% -> 0%
where the time goes in v1:
time: 67.9 us; the launch traced here: 67.7 us
  Pallas kernels  63.7 us (94%)
  local copies, waits for them, and re-layouts  3.33 us (5%)
    pallas_call x1, Pallas kernels, step(): pl.pallas_call(functools.partial(kernel, T, n, C), out_shape=(out, out),...  63.7 us
    reshape x2, local copies, waits for them, and re-layouts, step(): return (f.reshape(cols, rows).T[None], a.reshape(cols, rows).T[None])  3.33 us

profile of v1, /device:TPU:0, one launch (start us, length us, event | category | flops | bytes accessed | tf_op | source)
XLA Modules:
  0.0 67.7 jit_solution(11993526070367744304)
XLA Ops:
  0.6 63.7 %shard_map.50 = (bf16[4,32,512]{2,1,0:T(8,128)(2,1)}, bf16[4,32,512]{2,1,0:T(8,128)(2,1)}) custom-call(bf16[1,512,128]{2,1,0:T(8,128)(2,1)} %inc_ref.1, bf16[1,512,2048]{2,1,0:T(8,128)(2,1)} %p_hbm.1, f32[1,512]{1,0:T(1,128)} %w_ref.1), custom_call_target="tpu_custom_call" | custom-call | tf_op jit(solution)/shard_map/pallas_call | solution.py:164
  64.4 1.7 %copy.5 = bf16[128,512]{0,1:T(8,128)(2,1)} copy(bf16[128,512]{1,0:T(8,128)(2,1)} %bitcast.11) | data formatting | bytes 262144 | tf_op jit(solution)/shard_map/reshape | solution.py:183
  66.0 1.7 %copy.6 = bf16[128,512]{0,1:T(8,128)(2,1)} copy(bf16[128,512]{1,0:T(8,128)(2,1)} %bitcast.10) | data formatting | bytes 262144 | tf_op jit(solution)/shard_map/reshape | solution.py:183

commit v2 on v1

--- a/solution.py
+++ b/solution.py
@@ -8,7 +8,7 @@
 from jax.sharding import PartitionSpec as P
 
 MESH = pl.DeviceIdType.MESH
-CHUNK = 32
+CHUNK = 16
 
 
 def partner(s, d, n):
@@ -22,7 +22,8 @@
     return out
 
 
-def kernel(T, n, C, inc_ref, p_hbm, w_ref, f_ref, a_ref, p, pt, x, r, q, p_sem, fs, fr, bs, br):
+def kernel(T, n, C, inc_hbm, p_hbm, w_hbm, f_hbm, a_hbm, inc_ref, w_ref, f_ref, a_ref, whole, p, pt, x, r, q,
+           in_sem, out_sem, p_sem, fs, fr, bs, br):
     t, s = lax.axis_index("tm"), lax.axis_index("state")
     rows, dim = p.shape
     parts = p_sem.shape[0]
@@ -32,6 +33,10 @@
         cut = pl.ds(i * part, part)
         return pltpu.make_async_copy(p_hbm.at[0, cut, :], p.at[cut, :], p_sem.at[i])
 
+    inc_load = pltpu.make_async_copy(inc_hbm.at[0], inc_ref, in_sem.at[0])
+    w_load = pltpu.make_async_copy(w_hbm, w_ref, in_sem.at[1])
+    inc_load.start()
+    w_load.start()
     for i in range(parts):
         load(i).start()
 
@@ -51,7 +56,8 @@
             pl.semaphore_signal(barrier, inc=1, device_id=(other, j), device_id_type=MESH)
 
     neighbours(greet)
-    turned = inc_ref[0].T
+    inc_load.wait()
+    turned = inc_ref[...].T
     for c in range(C):
         f_ref[c] = turned[c * CHUNK:(c + 1) * CHUNK, :]
     middle = jnp.logical_and(t > 0, t < T - 1)
@@ -73,6 +79,12 @@
         return pltpu.make_async_remote_copy(
             src_ref=q.at[c, d], dst_ref=r.at[c, index], send_sem=bs.at[c, d],
             recv_sem=br.at[c, index], device_id=to, device_id_type=MESH)
+
+    def store(k, source, target):
+        for c in range(C):
+            joined = source[c] if c == 0 else jnp.concatenate([joined, source[c]], axis=0)
+        whole[k] = joined.T
+        return pltpu.make_async_copy(whole.at[k], target.at[0], out_sem.at[k])
 
     def forward_send(c):
         @pl.when(t < T - 1)
@@ -98,6 +110,8 @@
                 term = jnp.dot(current, p[:, cut], preferred_element_type=jnp.float32)
                 q[c, d] = term.astype(jnp.bfloat16)
                 backward_copy(c, d, s, (t - 1, j)).start()
+
+    w_load.wait()
 
     @pl.when(t == 0)
     def _():
@@ -134,11 +148,17 @@
             def _():
                 backward(c, True)
 
+    f_store = store(0, f_ref, f_hbm)
+    f_store.start()
+
     @pl.when(t < T - 1)
     def _():
         @pl.loop(0, C)
         def _(c):
             backward(c, False)
+
+    a_store = store(1, a_ref, a_hbm)
+    a_store.start()
 
     @pl.loop(0, C)
     def _(c):
@@ -151,6 +171,9 @@
             def _():
                 backward_copy(c, d, s, (t, s)).wait_send()
 
+    f_store.wait()
+    a_store.wait()
+
 
 def solution(mesh):
     T, n = mesh.shape["tm"], mesh.shape["state"]
@@ -159,19 +182,26 @@
         _, rows, cols = increments.shape
         dim = propagators.shape[2]
         C = cols // CHUNK
-        out = jax.ShapeDtypeStruct((C, CHUNK, rows), jnp.bfloat16)
-        vmem = pl.BlockSpec(memory_space=pltpu.VMEM)
-        f, a = pl.pallas_call(
+        out = jax.ShapeDtypeStruct((1, rows, cols), jnp.bfloat16)
+        hbm = pl.BlockSpec(memory_space=pl.ANY)
+        return pl.pallas_call(
             functools.partial(kernel, T, n, C),
             out_shape=(out, out),
-            in_specs=[vmem, pl.BlockSpec(memory_space=pl.ANY), vmem],
-            out_specs=(vmem, vmem),
+            in_specs=[hbm] * 3,
+            out_specs=(hbm, hbm),
             scratch_shapes=[
+                pltpu.VMEM((rows, cols), jnp.bfloat16),
+                pltpu.VMEM((1, rows), jnp.float32),
+                pltpu.VMEM((C, CHUNK, rows), jnp.bfloat16),
+                pltpu.VMEM((C, CHUNK, rows), jnp.bfloat16),
+                pltpu.VMEM((2, rows, cols), jnp.bfloat16),
                 pltpu.VMEM((rows, dim), jnp.bfloat16),
                 pltpu.VMEM((dim, rows), jnp.bfloat16),
                 pltpu.VMEM((C, n, CHUNK, rows), jnp.bfloat16),
                 pltpu.VMEM((C, n, CHUNK, rows), jnp.bfloat16),
                 pltpu.VMEM((C, n, CHUNK, rows), jnp.bfloat16),
+                pltpu.SemaphoreType.DMA((2,)),
+                pltpu.SemaphoreType.DMA((2,)),
                 pltpu.SemaphoreType.DMA((4,)),
                 pltpu.SemaphoreType.DMA((C, n)),
                 pltpu.SemaphoreType.DMA((C, n)),
@@ -180,7 +210,6 @@
             ],
             compiler_params=pltpu.CompilerParams(collective_id=0, has_side_effects=True),
         )(increments, propagators, inv_var)
-        return (f.reshape(cols, rows).T[None], a.reshape(cols, rows).T[None])
 
     return jax.shard_map(
         step, mesh=mesh,

time: 67.9 us -> 63.1 us (0.929)
  Pallas kernels: 63.7 us -> 59.2 us
    pallas_call x1, Pallas kernels: 63.7 us -> 59.2 us  [step(): pl.pallas_call(functools.partial(kernel, T, n, C), out_shape=(out, out),...]
    reshape x2 -> x0, local copies, waits for them, and re-layouts: 3.33 us -> none  [step(): return (f.reshape(cols, rows).T[None], a.reshape(cols, rows).T[None])]
    unnamed x0 -> x2, local copies, waits for them, and re-layouts: none -> 3.14 us
where the time goes in v2:
time: 63.1 us; the launch traced here: 62.9 us
  Pallas kernels  59.2 us (94%)
  local copies, waits for them, and re-layouts  3.14 us (5%)
  between operations  0.64 us (1%)
    pallas_call x1, Pallas kernels, step(): pl.pallas_call(functools.partial(kernel, T, n, C), out_shape=(out, out),...  59.2 us
    unnamed x2, local copies, waits for them, and re-layouts  3.14 us

profile of v2, /device:TPU:0, one launch (start us, length us, event | category | flops | bytes accessed | tf_op | source)
XLA Modules:
  0.0 62.9 jit_solution(17265491203080670794)
XLA Ops:
  0.6 59.2 %shard_map.50 = (bf16[1,512,128]{2,1,0:T(8,128)(2,1)}, bf16[1,512,128]{2,1,0:T(8,128)(2,1)}) custom-call(bf16[1,512,128]{2,1,0:T(8,128)(2,1)} %inc_hbm.1, bf16[1,512,2048]{2,1,0:T(8,128)(2,1)} %p_hbm.1, f32[1,512]{1,0:T(1,128)} %w_hbm.1), custom_call_target="tpu_custom_call" | custom-call | tf_op jit(solution)/shard_map/pallas_call | solution.py:187
  59.8 1.6 %copy.7 = bf16[1,512,128]{2,1,0:T(8,128)(2,1)} copy(bf16[1,512,128]{2,1,0:T(8,128)(2,1)} %get-tuple-element.4) | data formatting | bytes 262144
  61.4 1.6 %copy.8 = bf16[1,512,128]{2,1,0:T(8,128)(2,1)} copy(bf16[1,512,128]{2,1,0:T(8,128)(2,1)} %get-tuple-element.5) | data formatting | bytes 262144

commit v3 on v2

--- a/solution.py
+++ b/solution.py
@@ -92,24 +92,54 @@
             for d in reversed(range(n)):
                 forward_copy(c, d, s, (t + 1, partner(s, d, n))).start()
 
-    def backward(c, last):
-        weighted = w_ref[...] * f_ref[c].astype(jnp.float32)
+    def stacked(blocks):
+        return blocks[0] if len(blocks) == 1 else jnp.concatenate(blocks, axis=0)
+
+    def forward(cs):
+        total = stacked([f_ref[c] for c in cs]).astype(jnp.float32)
+        for d in range(n):
+            j = partner(s, d, n)
+            for c in cs:
+                forward_copy(c, d, j, (t, s)).wait_recv()
+            cut = pl.ds(pl.multiple_of(j * rows, rows), rows)
+            total += jnp.dot(stacked([x[c, j] for c in cs]), pt[cut, :], preferred_element_type=jnp.float32)
+        current = total.astype(jnp.bfloat16)
+        for k, c in enumerate(cs):
+            f_ref[c] = current[k * CHUNK:(k + 1) * CHUNK, :]
+
+    def backward(cs, last):
+        weighted = w_ref[...] * stacked([f_ref[c] for c in cs]).astype(jnp.float32)
         if not last:
             for d in range(n):
                 j = partner(s, d, n)
-                backward_copy(c, d, j, (t, s)).wait_recv()
-                weighted += r[c, j].astype(jnp.float32)
+                for c in cs:
+                    backward_copy(c, d, j, (t, s)).wait_recv()
+                weighted += stacked([r[c, j] for c in cs]).astype(jnp.float32)
         current = weighted.astype(jnp.bfloat16)
-        a_ref[c] = current
+        for k, c in enumerate(cs):
+            a_ref[c] = current[k * CHUNK:(k + 1) * CHUNK, :]
 
         @pl.when(t > 0)
         def _():
-            for d in reversed(range(n)):
-                j = partner(s, d, n)
-                cut = pl.ds(pl.multiple_of(j * rows, rows), rows)
-                term = jnp.dot(current, p[:, cut], preferred_element_type=jnp.float32)
-                q[c, d] = term.astype(jnp.bfloat16)
-                backward_copy(c, d, s, (t - 1, j)).start()
+            def term(d):
+                cut = pl.ds(pl.multiple_of(partner(s, d, n) * rows, rows), rows)
+                return jnp.dot(current, p[:, cut], preferred_element_type=jnp.float32).astype(jnp.bfloat16)
+
+            def send(d, value):
+                for k, c in enumerate(cs):
+                    q[c, d] = value[k * CHUNK:(k + 1) * CHUNK, :]
+                    backward_copy(c, d, s, (t - 1, partner(s, d, n))).start()
+
+            ready = term(n - 1)
+            for d in reversed(range(n - 1)):
+                following = term(d)
+                send(d + 1, ready)
+                ready = following
+            send(0, ready)
+
+    def turn(cs):
+        forward(cs)
+        backward(cs, True)
 
     w_load.wait()
 
@@ -133,29 +163,33 @@
             cut = pl.ds(pl.multiple_of(i * block, block), block)
             pt[cut, :] = p[:, cut].T
 
+        @pl.when(t < T - 1)
+        def _():
+            @pl.loop(0, C)
+            def _(c):
+                forward([c])
+                forward_send(c)
+
+        @pl.when(t == T - 1)
+        def _():
+            pairs = (C - 2) // 2
+            turn([0])
+
+            @pl.loop(0, pairs)
+            def _(i):
+                turn([1 + 2 * i, 2 + 2 * i])
+
+            for c in range(1 + 2 * pairs, C):
+                turn([c])
+
+    f_store = store(0, f_ref, f_hbm)
+    f_store.start()
+
+    @pl.when(t < T - 1)
+    def _():
         @pl.loop(0, C)
         def _(c):
-            total = f_ref[c].astype(jnp.float32)
-            for d in range(n):
-                j = partner(s, d, n)
-                forward_copy(c, d, j, (t, s)).wait_recv()
-                cut = pl.ds(pl.multiple_of(j * rows, rows), rows)
-                total += jnp.dot(x[c, j], pt[cut, :], preferred_element_type=jnp.float32)
-            f_ref[c] = total.astype(jnp.bfloat16)
-            forward_send(c)
-
-            @pl.when(t == T - 1)
-            def _():
-                backward(c, True)
-
-    f_store = store(0, f_ref, f_hbm)
-    f_store.start()
-
-    @pl.when(t < T - 1)
-    def _():
-        @pl.loop(0, C)
-        def _(c):
-            backward(c, False)
+            backward([c], False)
 
     a_store = store(1, a_ref, a_hbm)
     a_store.start()
@@ -175,6 +209,19 @@
     a_store.wait()
 
 
+def hand_on(f_in, a_in, f_out, a_out, buffer, sems):
+    pairs = ((f_in, f_out), (a_in, a_out))
+    loads = [pltpu.make_async_copy(src, buffer.at[k], sems.at[k]) for k, (src, _) in enumerate(pairs)]
+    stores = [pltpu.make_async_copy(buffer.at[k], dst, sems.at[2 + k]) for k, (_, dst) in enumerate(pairs)]
+    for load in loads:
+        load.start()
+    for load, store in zip(loads, stores):
+        load.wait()
+        store.start()
+    for store in stores:
+        store.wait()
+
+
 def solution(mesh):
     T, n = mesh.shape["tm"], mesh.shape["state"]
 
@@ -184,7 +231,7 @@
         C = cols // CHUNK
         out = jax.ShapeDtypeStruct((1, rows, cols), jnp.bfloat16)
         hbm = pl.BlockSpec(memory_space=pl.ANY)
-        return pl.pallas_call(
+        f, a = pl.pallas_call(
             functools.partial(kernel, T, n, C),
             out_shape=(out, out),
             in_specs=[hbm] * 3,
@@ -210,6 +257,13 @@
             ],
             compiler_params=pltpu.CompilerParams(collective_id=0, has_side_effects=True),
         )(increments, propagators, inv_var)
+        return pl.pallas_call(
+            hand_on,
+            out_shape=(out, out),
+            in_specs=[hbm] * 2,
+            out_specs=(hbm, hbm),
+            scratch_shapes=[pltpu.VMEM((2, 1, rows, cols), jnp.bfloat16), pltpu.SemaphoreType.DMA((4,))],
+        )(f, a)
 
     return jax.shard_map(
         step, mesh=mesh,

time: 63.1 us -> 59.8 us (0.948)
  local copies, waits for them, and re-layouts: 3.14 us -> 0 us
    unnamed x2 -> x0, local copies, waits for them, and re-layouts: 3.14 us -> none
    pallas_call x1, Pallas kernels: 59.2 us -> 57.3 us  [step(): pl.pallas_call(functools.partial(kernel, T, n, C), out_shape=(out, out),...]
    pallas_call x0 -> x1, Pallas kernels: none -> 1.66 us  [step(): pl.pallas_call(hand_on, out_shape=(out, out), in_specs=[hbm] * 2, out_spe...]
where the time goes in v3:
time: 59.8 us; the launch traced here: 59.6 us
  Pallas kernels  59 us (99%)
  between operations  0.64 us (1%)
    pallas_call x1, Pallas kernels, step(): pl.pallas_call(functools.partial(kernel, T, n, C), out_shape=(out, out),...  57.3 us
    pallas_call x1, Pallas kernels, step(): pl.pallas_call(hand_on, out_shape=(out, out), in_specs=[hbm] * 2, out_spe...  1.66 us

profile of v3, /device:TPU:0, one launch (start us, length us, event | category | flops | bytes accessed | tf_op | source)
XLA Modules:
  0.0 59.6 jit_solution(10718953065504934722)
XLA Ops:
  0.6 57.3 %shard_map.50 = (bf16[1,512,128]{2,1,0:T(8,128)(2,1)}, bf16[1,512,128]{2,1,0:T(8,128)(2,1)}) custom-call(bf16[1,512,128]{2,1,0:T(8,128)(2,1)} %inc_hbm.1, bf16[1,512,2048]{2,1,0:T(8,128)(2,1)} %p_hbm.1, f32[1,512]{1,0:T(1,128)} %w_hbm.1), custom_call_target="tpu_custom_call" | custom-call | tf_op jit(solution)/shard_map/pallas_call | solution.py:234
  58.0 1.7 %shard_map.51 = (bf16[1,512,128]{2,1,0:T(8,128)(2,1)}, bf16[1,512,128]{2,1,0:T(8,128)(2,1)}) custom-call(bf16[1,512,128]{2,1,0:T(8,128)(2,1)} %get-tuple-element.4.f_in, bf16[1,512,128]{2,1,0:T(8,128)(2,1)} %get-tuple-element.5.a_in), custom_call_target="tpu_custom_call" | custom-call | tf_op jit(solution)/shard_map/pallas_call | solution.py:260
